TPU v7x, 32 devices: a whole 2x2x4 slice. The times are simulated.
32 devices in a mesh: freq: 4 (over z), trace: 8 (over y, x, core).
Axes of the slice: x: 2, y: 2, z: 4, core: 2. Of those that a mesh axis runs over, the one named last changes fastest.
Arguments:
- recorded: float32 [8, 2, 2048, 1024], P(None, None, 'freq', 'trace'), may hold values from -16 to 16
- multiples: float32 [8, 2, 2048, 1024], P(None, None, 'freq', 'trace'), may hold values from -6 to 6
Outputs:
- primaries: float32 [8, 2, 2048, 1024], P(None, None, 'freq', 'trace')
- filters: float32 [8, 2, 32, 64], P(None, None, 'freq')
All inputs are finite; a program needn't handle non-finite values.
Results may differ from a plain program's by a relative error of at most 0.0001.
Values sent between devices are 32-bit elements; how exact they have to be, the bound alone decides.
A program may use at most 128 MiB of HBM per device.

v0:
```python
import jax
import jax.numpy as jnp
from jax import lax
from jax.sharding import PartitionSpec as P

FB = 64
TAPS = 64
ITERS = 3


def with_halo(value, sides, width):
    for axis, dim in sides:
        size, length = (lax.axis_size(axis), value.shape[dim])
        up = [(i, (i + 1) % size) for i in range(size - 1)]
        down = [(j, i) for i, j in up]
        last = lax.slice_in_dim(value, length - width, length, axis=dim)
        first = lax.slice_in_dim(value, 0, width, axis=dim)
        before = lax.ppermute(last, axis, up)
        after = lax.ppermute(first, axis, down)
        value = jnp.concatenate([before, value, after], axis=dim)
    return value


def toeplitz_rows(taps_vec, trace_rows):
    tap_count = taps_vec.shape[-1]
    window_len = trace_rows + tap_count
    leading = taps_vec.shape[:-1]
    padded = jnp.concatenate(
        [
            jnp.zeros(leading + (1,), jnp.float32),
            taps_vec[..., ::-1],
            jnp.zeros(leading + (trace_rows,), jnp.float32),
        ],
        -1,
    )
    repeated = jnp.tile(padded, (1,) * len(leading) + (trace_rows,))
    return repeated[..., : trace_rows * window_len].reshape(leading + (trace_rows, window_len))


def product(left, right):
    return jnp.einsum("bfj,bxj->bfx", left, right, precision=lax.Precision.HIGHEST)


def correlate(left, right):
    return jnp.einsum("bfj,bfx->bxj", left, right, precision=lax.Precision.HIGHEST)


def forward_one(window, taps_vec):
    trace_rows = window.shape[-1] - taps_vec.shape[-1]
    toeplitz = toeplitz_rows(taps_vec, trace_rows)
    real_part = product(window[0], toeplitz[0]) - product(window[1], toeplitz[1])
    imag_part = product(window[0], toeplitz[1]) + product(window[1], toeplitz[0])
    return jnp.stack([real_part, imag_part])


def adjoint_one(window, residual, tap_count):
    real_part = correlate(window[0], residual[0]) + correlate(window[1], residual[1])
    imag_part = correlate(window[0], residual[1]) - correlate(window[1], residual[0])
    crossed = jnp.stack([real_part, imag_part])
    trace_rows, window_len = crossed.shape[-2:]
    leading = crossed.shape[:-2]
    flattened = crossed.reshape(leading + (trace_rows * window_len,))
    flattened = jnp.concatenate([flattened, jnp.zeros(leading + (trace_rows,), jnp.float32)], -1)
    column_sums = jnp.sum(flattened.reshape(leading + (trace_rows, window_len + 1)), axis=-2)
    return column_sums[..., 1 : tap_count + 1][..., ::-1]


def bending(edge_pad):
    return 2.0 * edge_pad[:, :, 1:-1] - edge_pad[:, :, :-2] - edge_pad[:, :, 2:]


def inner_sum(left, right):
    return jnp.sum(left * right, axis=(1, 2, 3))


def body(recorded, multiples):
    half_taps = TAPS // 2
    trace_rows = multiples.shape[3]
    edged = with_halo(multiples, (("trace", 3),), half_taps)
    shot_count, part_count, freq_rows, window_len = edged.shape
    block_count = freq_rows // FB
    windows = edged.reshape(shot_count, part_count, block_count, FB, window_len)
    trace_count = lax.axis_size("trace")
    weight = 0.5 * FB * trace_rows * trace_count
    residual = recorded
    shaping = jnp.zeros((shot_count, part_count, block_count, TAPS), jnp.float32)
    bent_sum = jnp.zeros_like(shaping)
    direction = shaping
    norm_now = jnp.ones((shot_count,), jnp.float32)
    for iteration in range(ITERS):
        pieces = residual.reshape(shot_count, part_count, block_count, FB, trace_rows)
        gradient = (
            lax.psum(
                lax.map(lambda paired: adjoint_one(paired[0], paired[1], TAPS), (windows, pieces)),
                "trace",
            )
            - bent_sum
        )
        norm_next = lax.psum(inner_sum(gradient, gradient), "freq")
        if iteration == 0:
            direction = gradient
        else:
            direction = gradient + (norm_next / norm_now)[:, None, None, None] * direction
        norm_now = norm_next
        result = lax.map(lambda paired: forward_one(paired[0], paired[1]), (windows, direction))
        applied = result.reshape(shot_count, part_count, freq_rows, trace_rows)
        edge_pad = with_halo(direction, (("freq", 2),), 1)
        smooth = weight * bending(edge_pad)
        energy_sum, smooth_sum = lax.psum(
            (jnp.sum(applied * applied, axis=(1, 2, 3)), inner_sum(direction, smooth)),
            ("freq", "trace"),
        )
        energy = energy_sum + smooth_sum / trace_count
        step_len = (norm_now / energy)[:, None, None, None]
        shaping = shaping + step_len * direction
        residual = residual - step_len * applied
        bent_sum = bent_sum + step_len * smooth
    return (residual, shaping)


def solution(mesh):
    return jax.shard_map(
        body,
        mesh=mesh,
        in_specs=(P(None, None, "freq", "trace"), P(None, None, "freq", "trace")),
        out_specs=(P(None, None, "freq", "trace"), P(None, None, "freq", None)),
        check_vma=False,
    )
```

profile of v0, /device:TPU:0, one launch (start us, length us, event | category | flops | bytes accessed | tf_op | source)
XLA Modules:
  0.0 1106.0 jit_solution(16259001931993445002)
XLA Ops:
  0.6 8.0 fusion.60
  8.6 2.8 copy.56
  13.9 2.8 copy.57
  23.4 3.7 copy.43
  27.1 8.8 pad_maximum_fusion
  35.8 140.7 %while.60 = (s32[]{:T(128)}, f32[8,2,8,64]{3,2,1,0:T(8,128)S(1)}, f32[8,2,8,64,128]{4,3,2,1,0:T(8,128)}, f32[8,2,8,64,192]{4,3,2,1,0:T(8,128)}, s32[]{:T(128)}, /*index=5*/s32[]{:T(128)}, s32[]{}, f32[]{:T(128)}) while((s32[]{:T(128)}, f32[8,2,8,64]{3,2,1,0:T(8,128)S(1)}, f32[8,2,8,64,128]{4,3,2,1,0:T(8,128)}, ...), condition=%wide.region_2.3_spmd, body=%wide.region_0.2_spmd.sunk | while | flops 606346240 | bytes 22103216 | solution.py:94
  48.9 4.2 reshape.130
  66.4 4.2 reshape.130
  84.0 4.2 reshape.130
  101.6 4.2 reshape.130
  119.2 4.2 reshape.130
  136.8 4.2 reshape.130
  154.3 4.2 reshape.130
  171.9 4.2 reshape.130
  176.5 40.3 %psum.84 = f32[8,2,8,64]{3,2,1,0:T(8,128)S(1)} all-reduce(f32[8,2,8,64]{3,2,1,0:T(8,128)S(1)} %get-tuple-element.134), channel_id=1, replica_groups=mesh['freq'=4,'trace'=8] {'trace'}, use_global_device_ids=true, to_apply=%region_3.4 | all-reduce | flops 8192 | bytes 65536 | tf_op jit(solution)/shard_map/psum | solution.py:93
  216.9 3.5 collective-permute-start.2
  224.4 120.3 %while.61 = (s32[]{:T(128)}, f32[8,2,8,64,128]{4,3,2,1,0:T(8,128)}, f32[8,2,8,64,192]{4,3,2,1,0:T(8,128)}, f32[8,2,8,64]{3,2,1,0:T(8,128)S(1)}, s32[]{:T(128)}, /*index=5*/f32[]{:T(128)}, f32[]{:T(128)}, s32[]{:T(128)}, s32[]{}) while((s32[]{:T(128)}, f32[8,2,8,64,128]{4,3,2,1,0:T(8,128)}, f32[8,2,8,64,192]{4,3,2,1,0:T(8,128)}, ...), condition=%wide.region_7.8_spmd, body=%wide.region_6.7_spmd.sunk | while | flops 604248064 | bytes 18950932 | solution.py:105
  347.5 13.0 %psum.85 = f32[8]{0:T(128)S(1)} all-reduce(f32[8]{0:T(128)S(1)} %get-tuple-element.141), channel_id=1, replica_groups=mesh['freq'=4,'trace'=8] {'freq'}, use_global_device_ids=true, to_apply=%region_5.6 | all-reduce | flops 8 | bytes 64 | tf_op jit(solution)/shard_map/psum | solution.py:99
  360.5 37.8 %all-reduce.5 = (f32[8]{0:T(128)S(1)}, f32[8]{0:T(128)S(1)}) all-reduce(f32[8]{0:T(128)S(1)} %multiply_reduce_fusion.2, f32[8]{0:T(128)S(1)} %get-tuple-element.140), channel_id=1, replica_groups=mesh['freq'=4,'trace'=8] {'freq','trace'}, use_global_device_ids=true, to_apply=%region_9.10 | all-reduce | flops 16 | bytes 128 | tf_op jit(solution)/shard_map/psum | solution.py:109
  398.3 6.0 fusion.47
  404.3 140.6 %while.62 = (s32[]{:T(128)}, f32[8,2,8,64]{3,2,1,0:T(8,128)S(1)}, f32[8,2,8,64,128]{4,3,2,1,0:T(8,128)}, f32[8,2,8,64,192]{4,3,2,1,0:T(8,128)}, s32[]{:T(128)}, /*index=5*/s32[]{:T(128)}, s32[]{}, f32[]{:T(128)}) while((s32[]{:T(128)}, f32[8,2,8,64]{3,2,1,0:T(8,128)S(1)}, f32[8,2,8,64,128]{4,3,2,1,0:T(8,128)}, ...), condition=%wide.region_14.15_spmd, body=%wide.region_12.14_spmd.sunk | while | flops 606346240 | bytes 22103216 | solution.py:94
  417.3 4.2 reshape.131
  434.9 4.2 reshape.131
  452.5 4.2 reshape.131
  470.0 4.2 reshape.131
  487.6 4.2 reshape.131
  505.2 4.2 reshape.131
  522.8 4.2 reshape.131
  540.4 4.2 reshape.131
  544.9 23.8 %psum.88 = f32[8,2,8,64]{3,2,1,0:T(8,128)S(1)} all-reduce(f32[8,2,8,64]{3,2,1,0:T(8,128)S(1)} %get-tuple-element.136), channel_id=1, replica_groups=mesh['freq'=4,'trace'=8] {'trace'}, use_global_device_ids=true, to_apply=%region_15.16 | all-reduce | flops 8192 | bytes 65536 | tf_op jit(solution)/shard_map/psum | solution.py:93
  569.0 11.2 %psum.89 = f32[8]{0:T(128)S(1)} all-reduce(f32[8]{0:T(128)S(1)} %multiply_reduce_fusion.5), channel_id=1, replica_groups=mesh['freq'=4,'trace'=8] {'freq'}, use_global_device_ids=true, to_apply=%region_17.18 | all-reduce | flops 8 | bytes 64 | tf_op jit(solution)/shard_map/psum | solution.py:99
  585.9 120.0 %while.63 = (s32[]{:T(128)}, f32[8,2,8,64,128]{4,3,2,1,0:T(8,128)}, f32[8,2,8,64,192]{4,3,2,1,0:T(8,128)}, f32[8,2,8,64]{3,2,1,0:T(8,128)S(1)}, s32[]{:T(128)}, /*index=5*/f32[]{:T(128)}, f32[]{:T(128)}, s32[]{:T(128)}, s32[]{}) while((s32[]{:T(128)}, f32[8,2,8,64,128]{4,3,2,1,0:T(8,128)}, f32[8,2,8,64,192]{4,3,2,1,0:T(8,128)}, ...), condition=%wide.region_19.20_spmd, body=%wide.region_18.19_spmd.sunk | while | flops 604248064 | bytes 18950932 | solution.py:105
  708.8 40.5 %all-reduce.4 = (f32[8]{0:T(128)S(1)}, f32[8]{0:T(128)S(1)}) all-reduce(f32[8]{0:T(128)S(1)} %multiply_reduce_fusion.1, f32[8]{0:T(128)S(1)} %multiply_reduce_fusion.4), channel_id=1, replica_groups=mesh['freq'=4,'trace'=8] {'freq','trace'}, use_global_device_ids=true, to_apply=%region_21.22 | all-reduce | flops 16 | bytes 128 | tf_op jit(solution)/shard_map/psum | solution.py:109
  749.3 6.0 fusion.46
  755.3 140.6 %while.64 = (s32[]{:T(128)}, f32[8,2,8,64]{3,2,1,0:T(8,128)S(1)}, f32[8,2,8,64,128]{4,3,2,1,0:T(8,128)}, f32[8,2,8,64,192]{4,3,2,1,0:T(8,128)}, s32[]{:T(128)}, /*index=5*/s32[]{:T(128)}, s32[]{}, f32[]{:T(128)}) while((s32[]{:T(128)}, f32[8,2,8,64]{3,2,1,0:T(8,128)S(1)}, f32[8,2,8,64,128]{4,3,2,1,0:T(8,128)}, ...), condition=%wide.region_26.27_spmd, body=%wide.region_24.26_spmd.sunk | while | flops 606346240 | bytes 22103216 | solution.py:94
  768.3 4.2 reshape.132
  785.9 4.2 reshape.132
  803.5 4.2 reshape.132
  821.1 4.2 reshape.132
  838.6 4.2 reshape.132
  856.2 4.2 reshape.132
  873.8 4.2 reshape.132
  891.4 4.2 reshape.132
  896.0 23.5 %psum.92 = f32[8,2,8,64]{3,2,1,0:T(8,128)S(1)} all-reduce(f32[8,2,8,64]{3,2,1,0:T(8,128)S(1)} %get-tuple-element.138), channel_id=1, replica_groups=mesh['freq'=4,'trace'=8] {'trace'}, use_global_device_ids=true, to_apply=%region_27.28 | all-reduce | flops 8192 | bytes 65536 | tf_op jit(solution)/shard_map/psum | solution.py:93
  919.7 9.9 psum.93
  936.1 119.7 %while.65 = (s32[]{:T(128)}, f32[8,2,8,64,128]{4,3,2,1,0:T(8,128)}, f32[8,2,8,64,192]{4,3,2,1,0:T(8,128)}, f32[8,2,8,64]{3,2,1,0:T(8,128)S(1)}, s32[]{:T(128)}, /*index=5*/f32[]{:T(128)}, f32[]{:T(128)}, s32[]{:T(128)}, s32[]{}) while((s32[]{:T(128)}, f32[8,2,8,64,128]{4,3,2,1,0:T(8,128)}, f32[8,2,8,64,192]{4,3,2,1,0:T(8,128)}, ...), condition=%wide.region_31.32_spmd, body=%wide.region_30.31_spmd.sunk | while | flops 604248064 | bytes 18950932 | solution.py:105
  1058.7 40.3 %all-reduce.3 = (f32[8]{0:T(128)S(1)}, f32[8]{0:T(128)S(1)}) all-reduce(f32[8]{0:T(128)S(1)} %multiply_reduce_fusion, f32[8]{0:T(128)S(1)} %fusion.51), channel_id=1, replica_groups=mesh['freq'=4,'trace'=8] {'freq','trace'}, use_global_device_ids=true, to_apply=%region_33.34 | all-reduce | flops 16 | bytes 128 | tf_op jit(solution)/shard_map/psum | solution.py:109
  1099.7 6.1 fusion.45
  (737 shorter events, 711.8 us)
Async XLA Ops:
  11.4 6.8 collective-permute-start
  16.7 6.7 collective-permute-start.1
  216.9 130.4 %collective-permute-start.2 = (f32[8,2,1,64]{3,2,1,0:T(1,128)S(1)}, f32[8,2,1,64]{3,2,1,0:T(1,128)S(1)}, u32[]{:S(2)}, u32[]{:S(2)}) collective-permute-start(f32[8,2,1,64]{3,2,1,0:T(1,128)S(1)} %get-tuple-element.214), channel_id=1, source_target_pairs={{0,8},{8,16},{16,24},{1,9},{9,17},{17,25},{2,10},{10,18},{18,26},{... | collective-permute-start | bytes 12296 | tf_op jit(solution)/shard_map/ppermute | solution.py:18
  220.3 126.9 %collective-permute-start.3 = (f32[8,2,1,64]{3,2,1,0:T(1,128)S(1)}, f32[8,2,1,64]{3,2,1,0:T(1,128)S(1)}, u32[]{:S(2)}, u32[]{:S(2)}) collective-permute-start(f32[8,2,1,64]{3,2,1,0:T(1,128)S(1)} %get-tuple-element.215), channel_id=1, source_target_pairs={{8,0},{16,8},{24,16},{9,1},{17,9},{25,17},{10,2},{18,10},{26,18},{... | collective-permute-start | bytes 12296 | tf_op jit(solution)/shard_map/ppermute | solution.py:19
  580.3 128.3 %collective-permute-start.4 = (f32[8,2,1,64]{3,2,1,0:T(1,128)S(1)}, f32[8,2,1,64]{3,2,1,0:T(1,128)S(1)}, u32[]{:S(2)}, u32[]{:S(2)}) collective-permute-start(f32[8,2,1,64]{3,2,1,0:T(1,128)S(1)} %get-tuple-element.212), channel_id=1, source_target_pairs={{0,8},{8,16},{16,24},{1,9},{9,17},{17,25},{2,10},{10,18},{18,26},{... | collective-permute-start | bytes 12296 | tf_op jit(solution)/shard_map/ppermute | solution.py:18
  581.9 126.7 %collective-permute-start.5 = (f32[8,2,1,64]{3,2,1,0:T(1,128)S(1)}, f32[8,2,1,64]{3,2,1,0:T(1,128)S(1)}, u32[]{:S(2)}, u32[]{:S(2)}) collective-permute-start(f32[8,2,1,64]{3,2,1,0:T(1,128)S(1)} %get-tuple-element.213), channel_id=1, source_target_pairs={{8,0},{16,8},{24,16},{9,1},{17,9},{25,17},{10,2},{18,10},{26,18},{... | collective-permute-start | bytes 12296 | tf_op jit(solution)/shard_map/ppermute | solution.py:19
  929.8 128.7 %collective-permute-start.6 = (f32[8,2,1,64]{3,2,1,0:T(1,128)S(1)}, f32[8,2,1,64]{3,2,1,0:T(1,128)S(1)}, u32[]{:S(2)}, u32[]{:S(2)}) collective-permute-start(f32[8,2,1,64]{3,2,1,0:T(1,128)S(1)} %get-tuple-element.210), channel_id=1, source_target_pairs={{0,8},{8,16},{16,24},{1,9},{9,17},{17,25},{2,10},{10,18},{18,26},{... | collective-permute-start | bytes 12296 | tf_op jit(solution)/shard_map/ppermute | solution.py:18
  932.1 126.4 %collective-permute-start.7 = (f32[8,2,1,64]{3,2,1,0:T(1,128)S(1)}, f32[8,2,1,64]{3,2,1,0:T(1,128)S(1)}, u32[]{:S(2)}, u32[]{:S(2)}) collective-permute-start(f32[8,2,1,64]{3,2,1,0:T(1,128)S(1)} %get-tuple-element.211), channel_id=1, source_target_pairs={{8,0},{16,8},{24,16},{9,1},{17,9},{25,17},{10,2},{18,10},{26,18},{... | collective-permute-start | bytes 12296 | tf_op jit(solution)/shard_map/ppermute | solution.py:19
where the time goes:
time: 1120 us; the launch traced here: 1110 us
  matrix products  463 us (41%)
  local copies, waits for them, and re-layouts  287 us (26%)
  blocking collectives  240 us (21%)
  other arithmetic  93.1 us (8%)
  starting transfers between devices  15.8 us (1%)
    dot_general x96, matrix products, correlate(): jnp.einsum('bfj,bfx->bxj', left, right, precision=lax.Precision.HIGHEST)  246 us
    dot_general x96, matrix products, product(): jnp.einsum('bfj,bxj->bfx', left, right, precision=lax.Precision.HIGHEST)  217 us
    psum x3, blocking collectives, body(): lax.psum((jnp.sum(applied * applied, axis=(1, 2, 3)), inner_sum(direction...  119 us
    reshape x24, local copies, waits for them, and re-layouts, adjoint_one(): flattened.reshape(leading + (trace_rows, window_len + 1))  102 us
    psum x3, blocking collectives, body(): lax.psum(lax.map(lambda paired: adjoint_one(paired[0], paired[1], TAPS),...  87.7 us
    another operation x48, local copies, waits for them, and re-layouts, toeplitz_rows(): repeated = jnp.tile(padded, (1,) * len(leading) + (trace_rows,))  57.1 us
    slice x24, local copies, waits for them, and re-layouts, forward_one(): toeplitz[0]  35.3 us
    psum x3, blocking collectives, body(): norm_next = lax.psum(inner_sum(gradient, gradient), 'freq')  34.1 us
  transfers between devices with their start and end apart: 8, of which 1 were waited for; matrix products, arithmetic and copies ran while one was open for 34% of the time, Pallas kernels for 0%

commit v1 on v0

--- a/solution.py
+++ b/solution.py
@@ -90,9 +90,14 @@
     for iteration in range(ITERS):
         pieces = residual.reshape(shot_count, part_count, block_count, FB, trace_rows)
         gradient = (
-            lax.psum(
-                lax.map(lambda paired: adjoint_one(paired[0], paired[1], TAPS), (windows, pieces)),
-                "trace",
+            jnp.sum(
+                lax.all_gather(
+                    lax.map(
+                        lambda paired: adjoint_one(paired[0], paired[1], TAPS), (windows, pieces)
+                    ),
+                    "trace",
+                ),
+                axis=0,
             )
             - bent_sum
         )

time: 1120 us -> 1080 us (0.964)
  blocking collectives: 240 us -> 200 us
    psum x3 -> x0, blocking collectives: 87.7 us -> none  [body(): lax.psum(lax.map(lambda paired: adjoint_one(paired[0], paired[1], TAPS),...]
    all_gather x0 -> x3, blocking collectives: none -> 47.8 us  [body(): lax.all_gather(lax.map(lambda paired: adjoint_one(paired[0], paired[1], T...]
  transfers between devices with their start and end apart: 8 -> 8, of which waited for: 1 -> 1; matrix products, arithmetic and copies ran while one was open for 34% -> 36% of each run, Pallas kernels for 0% -> 0%
where the time goes in v1:
time: 1080 us; the launch traced here: 1070 us
  matrix products  463 us (43%)
  local copies, waits for them, and re-layouts  287 us (27%)
  blocking collectives  200 us (19%)
  other arithmetic  93.2 us (9%)
  starting transfers between devices  15.6 us (1%)
    dot_general x96, matrix products, correlate(): jnp.einsum('bfj,bfx->bxj', left, right, precision=lax.Precision.HIGHEST)  246 us
    dot_general x96, matrix products, product(): jnp.einsum('bfj,bxj->bfx', left, right, precision=lax.Precision.HIGHEST)  217 us
    psum x3, blocking collectives, body(): lax.psum((jnp.sum(applied * applied, axis=(1, 2, 3)), inner_sum(direction...  118 us
    reshape x24, local copies, waits for them, and re-layouts, adjoint_one(): flattened.reshape(leading + (trace_rows, window_len + 1))  102 us
    another operation x48, local copies, waits for them, and re-layouts, toeplitz_rows(): repeated = jnp.tile(padded, (1,) * len(leading) + (trace_rows,))  57.1 us
    all_gather x3, blocking collectives, body(): lax.all_gather(lax.map(lambda paired: adjoint_one(paired[0], paired[1], T...  47.8 us
    slice x24, local copies, waits for them, and re-layouts, forward_one(): toeplitz[0]  35.3 us
    psum x3, blocking collectives, body(): norm_next = lax.psum(inner_sum(gradient, gradient), 'freq')  34.2 us
  transfers between devices with their start and end apart: 8, of which 1 were waited for; matrix products, arithmetic and copies ran while one was open for 36% of the time, Pallas kernels for 0%

profile of v1, /device:TPU:0, one launch (start us, length us, event | category | flops | bytes accessed | tf_op | source)
XLA Modules:
  0.0 1065.5 jit_solution(9114947246544598918)
XLA Ops:
  0.6 8.0 fusion.60
  8.6 2.8 copy.56
  13.9 2.8 copy.57
  23.4 3.7 copy.43
  27.1 8.8 pad_maximum_fusion
  35.8 140.7 %while.60 = (s32[]{:T(128)}, f32[8,2,8,64]{3,2,1,0:T(8,128)S(1)}, f32[8,2,8,64,128]{4,3,2,1,0:T(8,128)}, f32[8,2,8,64,192]{4,3,2,1,0:T(8,128)}, s32[]{:T(128)}, /*index=5*/s32[]{:T(128)}, s32[]{}, f32[]{:T(128)}) while((s32[]{:T(128)}, f32[8,2,8,64]{3,2,1,0:T(8,128)S(1)}, f32[8,2,8,64,128]{4,3,2,1,0:T(8,128)}, ...), condition=%wide.region_2.3_spmd, body=%wide.region_0.2_spmd.sunk | while | flops 606346240 | bytes 22103216 | solution.py:95
  48.9 4.2 reshape.133
  66.4 4.2 reshape.133
  84.0 4.2 reshape.133
  101.6 4.2 reshape.133
  119.2 4.2 reshape.133
  136.8 4.2 reshape.133
  154.3 4.2 reshape.133
  171.9 4.2 reshape.133
  176.5 26.6 %all-gather = f32[64,2,8,64]{3,2,1,0:T(8,128)S(1)} all-gather(f32[8,2,8,64]{3,2,1,0:T(8,128)S(1)} %get-tuple-element.134), channel_id=2, replica_groups=mesh['freq'=4,'trace'=8] {'trace'}, dimensions={0}, use_global_device_ids=true | all-gather | bytes 294912 | tf_op jit(solution)/shard_map/all_gather | solution.py:94
  203.2 3.5 collective-permute-start.2
  210.5 120.3 %while.61 = (s32[]{:T(128)}, f32[8,2,8,64,128]{4,3,2,1,0:T(8,128)}, f32[8,2,8,64,192]{4,3,2,1,0:T(8,128)}, f32[8,2,8,64]{3,2,1,0:T(8,128)S(1)}, s32[]{:T(128)}, /*index=5*/f32[]{:T(128)}, f32[]{:T(128)}, s32[]{:T(128)}, s32[]{}) while((s32[]{:T(128)}, f32[8,2,8,64,128]{4,3,2,1,0:T(8,128)}, f32[8,2,8,64,192]{4,3,2,1,0:T(8,128)}, ...), condition=%wide.region_7.8_spmd, body=%wide.region_6.7_spmd.sunk | while | flops 604248064 | bytes 18950932 | solution.py:110
  333.6 13.1 %psum.63 = f32[8]{0:T(128)S(1)} all-reduce(f32[8]{0:T(128)S(1)} %get-tuple-element.141), channel_id=1, replica_groups=mesh['freq'=4,'trace'=8] {'freq'}, use_global_device_ids=true, to_apply=%region_5.6 | all-reduce | flops 8 | bytes 64 | tf_op jit(solution)/shard_map/psum | solution.py:104
  346.6 37.2 %all-reduce.5 = (f32[8]{0:T(128)S(1)}, f32[8]{0:T(128)S(1)}) all-reduce(f32[8]{0:T(128)S(1)} %multiply_reduce_fusion.2, f32[8]{0:T(128)S(1)} %get-tuple-element.140), channel_id=1, replica_groups=mesh['freq'=4,'trace'=8] {'freq','trace'}, use_global_device_ids=true, to_apply=%region_9.10 | all-reduce | flops 16 | bytes 128 | tf_op jit(solution)/shard_map/psum | solution.py:114
  383.9 6.0 fusion.47
  389.9 140.6 %while.62 = (s32[]{:T(128)}, f32[8,2,8,64]{3,2,1,0:T(8,128)S(1)}, f32[8,2,8,64,128]{4,3,2,1,0:T(8,128)}, f32[8,2,8,64,192]{4,3,2,1,0:T(8,128)}, s32[]{:T(128)}, /*index=5*/s32[]{:T(128)}, s32[]{}, f32[]{:T(128)}) while((s32[]{:T(128)}, f32[8,2,8,64]{3,2,1,0:T(8,128)S(1)}, f32[8,2,8,64,128]{4,3,2,1,0:T(8,128)}, ...), condition=%wide.region_14.15_spmd, body=%wide.region_12.14_spmd.sunk | while | flops 606346240 | bytes 22103216 | solution.py:95
  402.9 4.2 reshape.134
  420.5 4.2 reshape.134
  438.0 4.2 reshape.134
  455.6 4.2 reshape.134
  473.2 4.2 reshape.134
  490.8 4.2 reshape.134
  508.4 4.2 reshape.134
  525.9 4.2 reshape.134
  530.5 10.6 all-gather.1
  541.4 11.2 %psum.66 = f32[8]{0:T(128)S(1)} all-reduce(f32[8]{0:T(128)S(1)} %multiply_reduce_fusion.5), channel_id=1, replica_groups=mesh['freq'=4,'trace'=8] {'freq'}, use_global_device_ids=true, to_apply=%region_17.18 | all-reduce | flops 8 | bytes 64 | tf_op jit(solution)/shard_map/psum | solution.py:104
  558.3 120.0 %while.63 = (s32[]{:T(128)}, f32[8,2,8,64,128]{4,3,2,1,0:T(8,128)}, f32[8,2,8,64,192]{4,3,2,1,0:T(8,128)}, f32[8,2,8,64]{3,2,1,0:T(8,128)S(1)}, s32[]{:T(128)}, /*index=5*/f32[]{:T(128)}, f32[]{:T(128)}, s32[]{:T(128)}, s32[]{}) while((s32[]{:T(128)}, f32[8,2,8,64,128]{4,3,2,1,0:T(8,128)}, f32[8,2,8,64,192]{4,3,2,1,0:T(8,128)}, ...), condition=%wide.region_19.20_spmd, body=%wide.region_18.19_spmd.sunk | while | flops 604248064 | bytes 18950932 | solution.py:110
  681.2 40.5 %all-reduce.4 = (f32[8]{0:T(128)S(1)}, f32[8]{0:T(128)S(1)}) all-reduce(f32[8]{0:T(128)S(1)} %multiply_reduce_fusion.1, f32[8]{0:T(128)S(1)} %multiply_reduce_fusion.4), channel_id=1, replica_groups=mesh['freq'=4,'trace'=8] {'freq','trace'}, use_global_device_ids=true, to_apply=%region_21.22 | all-reduce | flops 16 | bytes 128 | tf_op jit(solution)/shard_map/psum | solution.py:114
  721.7 6.0 fusion.46
  727.7 140.6 %while.64 = (s32[]{:T(128)}, f32[8,2,8,64]{3,2,1,0:T(8,128)S(1)}, f32[8,2,8,64,128]{4,3,2,1,0:T(8,128)}, f32[8,2,8,64,192]{4,3,2,1,0:T(8,128)}, s32[]{:T(128)}, /*index=5*/s32[]{:T(128)}, s32[]{}, f32[]{:T(128)}) while((s32[]{:T(128)}, f32[8,2,8,64]{3,2,1,0:T(8,128)S(1)}, f32[8,2,8,64,128]{4,3,2,1,0:T(8,128)}, ...), condition=%wide.region_26.27_spmd, body=%wide.region_24.26_spmd.sunk | while | flops 606346240 | bytes 22103216 | solution.py:95
  740.7 4.2 reshape.135
  758.3 4.2 reshape.135
  775.9 4.2 reshape.135
  793.4 4.2 reshape.135
  811.0 4.2 reshape.135
  828.6 4.2 reshape.135
  846.2 4.2 reshape.135
  863.8 4.2 reshape.135
  868.3 10.6 all-gather.2
  879.2 9.9 psum.69
  895.6 119.7 %while.65 = (s32[]{:T(128)}, f32[8,2,8,64,128]{4,3,2,1,0:T(8,128)}, f32[8,2,8,64,192]{4,3,2,1,0:T(8,128)}, f32[8,2,8,64]{3,2,1,0:T(8,128)S(1)}, s32[]{:T(128)}, /*index=5*/f32[]{:T(128)}, f32[]{:T(128)}, s32[]{:T(128)}, s32[]{}) while((s32[]{:T(128)}, f32[8,2,8,64,128]{4,3,2,1,0:T(8,128)}, f32[8,2,8,64,192]{4,3,2,1,0:T(8,128)}, ...), condition=%wide.region_31.32_spmd, body=%wide.region_30.31_spmd.sunk | while | flops 604248064 | bytes 18950932 | solution.py:110
  1018.1 40.3 %all-reduce.3 = (f32[8]{0:T(128)S(1)}, f32[8]{0:T(128)S(1)}) all-reduce(f32[8]{0:T(128)S(1)} %multiply_reduce_fusion, f32[8]{0:T(128)S(1)} %fusion.51), channel_id=1, replica_groups=mesh['freq'=4,'trace'=8] {'freq','trace'}, use_global_device_ids=true, to_apply=%region_33.34 | all-reduce | flops 16 | bytes 128 | tf_op jit(solution)/shard_map/psum | solution.py:114
  1059.2 6.1 fusion.45
  (740 shorter events, 711.7 us)
Async XLA Ops:
  11.4 6.8 collective-permute-start
  16.7 6.7 collective-permute-start.1
  203.2 130.2 %collective-permute-start.2 = (f32[8,2,1,64]{3,2,1,0:T(1,128)S(1)}, f32[8,2,1,64]{3,2,1,0:T(1,128)S(1)}, u32[]{:S(2)}, u32[]{:S(2)}) collective-permute-start(f32[8,2,1,64]{3,2,1,0:T(1,128)S(1)} %get-tuple-element.214), channel_id=1, source_target_pairs={{0,8},{8,16},{16,24},{1,9},{9,17},{17,25},{2,10},{10,18},{18,26},{... | collective-permute-start | bytes 12296 | tf_op jit(solution)/shard_map/ppermute | solution.py:18
  206.7 126.7 %collective-permute-start.3 = (f32[8,2,1,64]{3,2,1,0:T(1,128)S(1)}, f32[8,2,1,64]{3,2,1,0:T(1,128)S(1)}, u32[]{:S(2)}, u32[]{:S(2)}) collective-permute-start(f32[8,2,1,64]{3,2,1,0:T(1,128)S(1)} %get-tuple-element.215), channel_id=1, source_target_pairs={{8,0},{16,8},{24,16},{9,1},{17,9},{25,17},{10,2},{18,10},{26,18},{... | collective-permute-start | bytes 12296 | tf_op jit(solution)/shard_map/ppermute | solution.py:19
  552.7 128.3 %collective-permute-start.4 = (f32[8,2,1,64]{3,2,1,0:T(1,128)S(1)}, f32[8,2,1,64]{3,2,1,0:T(1,128)S(1)}, u32[]{:S(2)}, u32[]{:S(2)}) collective-permute-start(f32[8,2,1,64]{3,2,1,0:T(1,128)S(1)} %get-tuple-element.212), channel_id=1, source_target_pairs={{0,8},{8,16},{16,24},{1,9},{9,17},{17,25},{2,10},{10,18},{18,26},{... | collective-permute-start | bytes 12296 | tf_op jit(solution)/shard_map/ppermute | solution.py:18
  554.3 126.7 %collective-permute-start.5 = (f32[8,2,1,64]{3,2,1,0:T(1,128)S(1)}, f32[8,2,1,64]{3,2,1,0:T(1,128)S(1)}, u32[]{:S(2)}, u32[]{:S(2)}) collective-permute-start(f32[8,2,1,64]{3,2,1,0:T(1,128)S(1)} %get-tuple-element.213), channel_id=1, source_target_pairs={{8,0},{16,8},{24,16},{9,1},{17,9},{25,17},{10,2},{18,10},{26,18},{... | collective-permute-start | bytes 12296 | tf_op jit(solution)/shard_map/ppermute | solution.py:19
  889.2 128.8 %collective-permute-start.6 = (f32[8,2,1,64]{3,2,1,0:T(1,128)S(1)}, f32[8,2,1,64]{3,2,1,0:T(1,128)S(1)}, u32[]{:S(2)}, u32[]{:S(2)}) collective-permute-start(f32[8,2,1,64]{3,2,1,0:T(1,128)S(1)} %get-tuple-element.210), channel_id=1, source_target_pairs={{0,8},{8,16},{16,24},{1,9},{9,17},{17,25},{2,10},{10,18},{18,26},{... | collective-permute-start | bytes 12296 | tf_op jit(solution)/shard_map/ppermute | solution.py:18
  891.6 126.4 %collective-permute-start.7 = (f32[8,2,1,64]{3,2,1,0:T(1,128)S(1)}, f32[8,2,1,64]{3,2,1,0:T(1,128)S(1)}, u32[]{:S(2)}, u32[]{:S(2)}) collective-permute-start(f32[8,2,1,64]{3,2,1,0:T(1,128)S(1)} %get-tuple-element.211), channel_id=1, source_target_pairs={{8,0},{16,8},{24,16},{9,1},{17,9},{25,17},{10,2},{18,10},{26,18},{... | collective-permute-start | bytes 12296 | tf_op jit(solution)/shard_map/ppermute | solution.py:19
